TPU v7x, 128 devices: a whole 4x4x4 slice. The times are simulated.
128 devices in a mesh: seq: 16 (over z, x), head: 8 (over y, core).
Axes of the slice: x: 4, y: 4, z: 4, core: 2. Of those that a mesh axis runs over, the one named last changes fastest.
Arguments:
- context: bfloat16 [32768, 2048], P('seq'), may hold values from -64 to 64
- wq_cross: bfloat16 [2048, 2048], P(None, 'head'), may hold values from -4 to 4
- wk_cross: bfloat16 [2048, 2048], P(None, 'head'), may hold values from -4 to 4
- wv_cross: bfloat16 [2048, 2048], P(None, 'head'), may hold values from -0.125 to 0.125
- wo_cross: bfloat16 [2048, 2048], P('head'), may hold values from -0.125 to 0.125
- wq_latent: bfloat16 [2048, 2048], P(None, 'head'), may hold values from -4 to 4
- wk_latent: bfloat16 [2048, 2048], P(None, 'head'), may hold values from -4 to 4
- wv_latent: bfloat16 [2048, 2048], P(None, 'head'), may hold values from -0.125 to 0.125
- wo_latent: bfloat16 [2048, 2048], P('head'), may hold values from -0.125 to 0.125
- cross_keep: int32 [16, 2048, 4096], P('head', None, 'seq'), may hold values from 0 to 255, as said below
- latent_keep: int32 [16, 2048, 128], P('head'), may hold values from 0 to 65535, as said below
- residual_keep: int32 [2, 2048, 128], replicated, may hold values from 0 to 65535, as said below
Outputs:
- latents_out: bfloat16 [2048, 2048], P('seq', 'head')
Inputs may be any that keep to these rules, and one draw needn't show every extreme that they name: `cross_keep`: each of the 8 low bits of a word is one keep flag, laid out as the steps say. `latent_keep`: each of the 16 low bits of a word is one keep flag, laid out as the steps say. `residual_keep`: each of the 16 low bits of a word is one keep flag, laid out as the steps say.
All inputs are finite; a program needn't handle non-finite values.
Results may differ from a plain program's by a relative error of at most 0.015.
Values may be sent and summed in bfloat16 or wider, within the bound.
No kernel may reach another device: no remote copies, remote signals or barrier semaphores. Data moves between devices by JAX's collectives and lax.ppermute only.
A program may use at most 128 MiB of HBM per device.

v0:
```python
import math
import jax
import jax.numpy as jnp
from jax import lax
from jax.sharding import PartitionSpec as P

keep_scale = 8.0 / 7.0
masked = -1e30


def from_root(value, axis, source):
    kept = jnp.where(lax.axis_index(axis) == source, value, 0).astype(value.dtype)
    return lax.psum(kept, axis)


def copy_for_each(value, axis):
    size = lax.axis_size(axis)
    return lax.all_to_all(
        jnp.broadcast_to(value[None], (size, *value.shape)), axis, 0, 0, tiled=True
    )


def of_everyone(value, axis):
    everything = copy_for_each(value, axis)
    return jnp.max(everything, axis=0)


def side_by_side(arrays, axis, dim, along):
    widths = [math.prod(a.shape[along:]) for a in arrays]
    both = jnp.concatenate(
        [a.reshape(*a.shape[:along], w) for a, w in zip(arrays, widths)], axis=along
    )
    filled = lax.psum_scatter(both, axis, scatter_dimension=dim, tiled=True)
    parts = jnp.split(filled, [sum(widths[:k]) for k in range(1, len(widths))], axis=along)
    return tuple(
        (b.reshape(*filled.shape[:along], *a.shape[along:]) for a, b in zip(arrays, parts))
    )


def in_blocks(value, dim, size):
    before, after = (value.shape[:dim], value.shape[dim + 1 :])
    return jnp.moveaxis(value.reshape(*before, size, -1, *after), dim, 0)


def sum_at_owner(value, axis, dim):
    parts = in_blocks(value, dim, lax.axis_size(axis))
    arrived = lax.all_to_all(parts, axis, split_axis=0, concat_axis=0, tiled=True)
    return arrived.astype(jnp.float32).sum(axis=0)


def of_everyone_2(value, axis):
    return copy_for_each(value, axis).sum(axis=0)


def laid_out(parts, dim):
    shape = list(parts.shape[1:])
    shape[dim] *= parts.shape[0]
    return jnp.moveaxis(parts, 0, dim).reshape(shape)


def gather_directly(value, axis, dim):
    parts = copy_for_each(value, axis)
    return laid_out(parts, dim)


def side_by_side_2(arrays, axis, dim, along):
    widths = [a.shape[along] for a in arrays]
    both = jnp.concatenate(arrays, axis=along)
    filled = lax.all_gather(both, axis, axis=dim, tiled=True)
    return tuple(jnp.split(filled, [sum(widths[:k]) for k in range(1, len(widths))], axis=along))


def unpack_bits(packed_words, word_bits):
    shifts = jnp.arange(word_bits, dtype=jnp.int32)
    bit_table = jnp.bitwise_and(jnp.right_shift(packed_words[..., None, :], shifts[:, None]), 1)
    return bit_table.reshape(packed_words.shape[:-1] + (word_bits * packed_words.shape[-1],))


def rms_rows(matrix):
    wide_rows = matrix.astype(jnp.float32)
    mean_square = jnp.mean(wide_rows * wide_rows, axis=-1, keepdims=True)
    return (wide_rows * lax.rsqrt(mean_square + 1e-06)).astype(jnp.bfloat16)


def per_device(
    context,
    wq_cross,
    wk_cross,
    wv_cross,
    wo_cross,
    wq_latent,
    wk_latent,
    wv_latent,
    wo_latent,
    cross_keep,
    latent_keep,
    residual_keep,
):
    seq_count = lax.axis_size("seq")
    seq_index = lax.axis_index("seq")
    head_index = lax.axis_index("head")
    tok_rows, model_width = context.shape
    head_local = cross_keep.shape[0]
    latent_count = cross_keep.shape[1]
    head_dim = wq_cross.shape[1] // head_local
    query_width = head_local * head_dim
    columns = model_width // lax.axis_size("head")
    local_rows = latent_count // seq_count
    score_scale = 1.0 / math.sqrt(head_dim)
    normed = rms_rows(context)
    key_rows = jnp.dot(normed, wk_cross, preferred_element_type=jnp.float32).astype(jnp.bfloat16)
    value_rows = jnp.dot(normed, wv_cross, preferred_element_type=jnp.float32).astype(jnp.bfloat16)
    own_queries = jnp.dot(normed, wq_cross, preferred_element_type=jnp.float32).astype(jnp.bfloat16)
    own_columns = lax.dynamic_slice_in_dim(context, head_index * columns, columns, 1)
    outgoing_rows = jnp.concatenate([own_queries, own_columns], axis=1)
    arrived_rows = from_root(outgoing_rows, "seq", seq_count - 1)
    queries = arrived_rows[:, :query_width]
    latent_context = arrived_rows[:, query_width:]
    first_latent = (seq_count - 1) * tok_rows
    block_rows = min(512, latent_count)
    block_count = latent_count // block_rows
    query_blocks = queries.reshape(block_count, block_rows, head_local, head_dim)
    mask_blocks = cross_keep.reshape(head_local, block_count, block_rows, -1).transpose(1, 0, 2, 3)
    key_heads = key_rows.reshape(tok_rows, head_local, head_dim)
    value_heads = value_rows.reshape(tok_rows, head_local, head_dim)
    key_pos = seq_index * tok_rows + jnp.arange(tok_rows, dtype=jnp.int32)

    def cross_block(block_items):
        query_block, mask_block, number = block_items
        scores = (
            jnp.einsum("qhd,khd->hqk", query_block, key_heads, preferred_element_type=jnp.float32)
            * score_scale
        )
        query_pos = first_latent + number * block_rows + jnp.arange(block_rows, dtype=jnp.int32)
        allowed = key_pos[None, None, :] <= query_pos[None, :, None]
        scores = jnp.where(allowed, scores, masked)
        row_top = jnp.max(scores, axis=-1)
        exponent = jnp.where(allowed, jnp.exp(scores - row_top[..., None]), 0.0)
        row_sum = jnp.sum(exponent, axis=-1)
        keep_flags = unpack_bits(mask_block, 8).astype(jnp.float32)
        weights = (exponent * keep_flags * keep_scale).astype(jnp.bfloat16)
        summed = jnp.einsum(
            "hqk,khd->hqd", weights, value_heads, preferred_element_type=jnp.float32
        )
        return (summed, row_top, row_sum)

    summed, row_top, row_sum = lax.map(
        cross_block, (query_blocks, mask_blocks, jnp.arange(block_count, dtype=jnp.int32))
    )
    summed = summed.transpose(1, 0, 2, 3).reshape(head_local, latent_count, head_dim)
    row_top = row_top.transpose(1, 0, 2).reshape(head_local, latent_count)
    row_sum = row_sum.transpose(1, 0, 2).reshape(head_local, latent_count)
    first_row = seq_index * local_rows
    row_peak = of_everyone(row_top, "seq")
    factor = jnp.exp(row_top - row_peak)
    numerator, denominator = tuple(
        (
            part.astype(jnp.float32)
            for part in side_by_side(
                (
                    (summed * factor[..., None]).astype(jnp.bfloat16),
                    (row_sum * factor).astype(jnp.bfloat16),
                ),
                "seq",
                1,
                2,
            )
        )
    )
    attended_heads = numerator / denominator[..., None]
    attended = (
        attended_heads.transpose(1, 0, 2)
        .reshape(local_rows, head_local * head_dim)
        .astype(jnp.bfloat16)
    )
    inputs = lax.dynamic_slice_in_dim(latent_context, first_row, local_rows, 0).astype(jnp.float32)
    residual_rows = lax.dynamic_slice_in_dim(residual_keep, first_row, local_rows, 1)
    residual_mask = lax.dynamic_slice_in_dim(
        unpack_bits(residual_rows, 16), head_index * columns, columns, 2
    ).astype(jnp.float32)
    branch = jnp.dot(attended, wo_cross, preferred_element_type=jnp.float32)
    branch = sum_at_owner(branch.astype(jnp.bfloat16), "head", 1)
    latents = (inputs + residual_mask[0] * keep_scale * branch).astype(jnp.bfloat16)
    wide_latents = latents.astype(jnp.float32)
    squares = of_everyone_2(jnp.sum(wide_latents * wide_latents, axis=-1), "head")
    normed_columns = (wide_latents * lax.rsqrt(squares / model_width + 1e-06)[:, None]).astype(
        jnp.bfloat16
    )
    normed_latents = gather_directly(normed_columns, "head", 1)
    latent_queries = jnp.dot(normed_latents, wq_latent, preferred_element_type=jnp.float32).astype(
        jnp.bfloat16
    )
    latent_keys = jnp.dot(normed_latents, wk_latent, preferred_element_type=jnp.float32).astype(
        jnp.bfloat16
    )
    latent_values = jnp.dot(normed_latents, wv_latent, preferred_element_type=jnp.float32).astype(
        jnp.bfloat16
    )
    my_index = first_row + jnp.arange(local_rows, dtype=jnp.int32)
    latent_words = lax.dynamic_slice_in_dim(latent_keep, first_row, local_rows, 1)
    latent_mask = unpack_bits(latent_words, 16).astype(jnp.float32)
    query_heads = latent_queries.reshape(local_rows, head_local, head_dim)
    initial = (
        jnp.zeros((head_local, local_rows, head_dim), jnp.float32),
        jnp.full((head_local, local_rows), masked, jnp.float32),
        jnp.zeros((head_local, local_rows), jnp.float32),
    )
    key_piece, value_piece = side_by_side_2((latent_keys, latent_values), "seq", 0, 1)
    piece_rows = key_piece.shape[0]
    key_index = jnp.arange(piece_rows, dtype=jnp.int32)

    def update(current):
        weighted, old_top, old_sum = current
        scores = (
            jnp.einsum(
                "qhd,khd->hqk",
                query_heads,
                key_piece.reshape(piece_rows, head_local, head_dim),
                preferred_element_type=jnp.float32,
            )
            * score_scale
        )
        allowed = key_index[None, None, :] <= my_index[None, :, None]
        scores = jnp.where(allowed, scores, masked)
        new_top = jnp.maximum(old_top, jnp.max(scores, axis=-1))
        exponent = jnp.where(allowed, jnp.exp(scores - new_top[..., None]), 0.0)
        keep_flags = jnp.take(latent_mask, key_index, axis=2)
        weights = (exponent * keep_flags * keep_scale).astype(jnp.bfloat16)
        added = jnp.einsum(
            "hqk,khd->hqd",
            weights,
            value_piece.reshape(piece_rows, head_local, head_dim),
            preferred_element_type=jnp.float32,
        )
        return (added, new_top, jnp.sum(exponent, axis=-1))

    needed = jnp.min(key_index) <= jnp.max(my_index)
    weighted, latent_top, latent_sum = lax.cond(needed, update, lambda current: current, initial)
    latent_attended = (
        (weighted / latent_sum[..., None])
        .transpose(1, 0, 2)
        .reshape(local_rows, head_local * head_dim)
        .astype(jnp.bfloat16)
    )
    latent_branch = jnp.dot(latent_attended, wo_latent, preferred_element_type=jnp.float32)
    latent_branch = sum_at_owner(latent_branch.astype(jnp.bfloat16), "head", 1)
    result = (wide_latents + residual_mask[1] * keep_scale * latent_branch).astype(jnp.bfloat16)
    return result


def solution(mesh):
    in_specs = (
        P("seq", None),
        P(None, "head"),
        P(None, "head"),
        P(None, "head"),
        P("head", None),
        P(None, "head"),
        P(None, "head"),
        P(None, "head"),
        P("head", None),
        P("head", None, "seq"),
        P("head", None, None),
        P(),
    )
    out_specs = P("seq", "head")
    return jax.shard_map(
        per_device, mesh=mesh, in_specs=in_specs, out_specs=out_specs, check_vma=False
    )
```

profile of v0, /device:TPU:1, one launch (start us, length us, event | category | flops | bytes accessed | tf_op | source)
XLA Modules:
  0.0 501.3 jit_solution(15853030671720512966)
XLA Ops:
  6.5 5.2 %fusion.31 = f32[2048]{0:T(1024)S(1)} fusion(bf16[2048,2048]{1,0:T(8,128)(2,1)} %param.16), kind=kLoop, calls=%fused_computation.50 | loop fusion | flops 12580864 | bytes 8396800 | tf_op jit(solution)/shard_map/reduce_sum | solution.py:81
  11.7 1.3 constant_dynamic-slice_fusion.2
  13.7 5.9 %convolution_convert_fusion.2 = bf16[2048,256]{0,1:T(8,128)(2,1)S(1)} fusion(bf16[2048,256]{1,0:T(8,128)(2,1)S(1)} %copy-done, bf16[2048,2048]{1,0:T(8,128)(2,1)} %param.16, f32[2048]{0:T(1024)S(1)} %add_rsqrt_fusion), kind=kOutput, calls=%fused_computation.54 | convolution fusion | flops 2160590848 | bytes 10493952 | tf_op jit(solution)/shard_map/dot_general | solution.py:113
  19.6 1.7 maximum_select_fusion
  21.6 6.2 %convolution_convert_fusion.1 = bf16[2048,256]{0,1:T(8,128)(2,1)S(1)} fusion(bf16[2048,256]{1,0:T(8,128)(2,1)} %param.18, bf16[2048,2048]{1,0:T(8,128)(2,1)} %param.16, f32[2048]{0:T(1024)S(1)} %add_rsqrt_fusion), kind=kOutput, calls=%fused_computation.53 | convolution fusion | flops 2160590848 | bytes 10493952 | tf_op jit(solution)/shard_map/dot_general | solution.py:111
  27.9 1.3 copy.130
  29.2 5.9 %convolution_convert_fusion = bf16[2048,256]{0,1:T(8,128)(2,1)S(1)} fusion(bf16[2048,256]{1,0:T(8,128)(2,1)S(1)} %copy-done.10, bf16[2048,2048]{1,0:T(8,128)(2,1)} %param.16, f32[2048]{0:T(1024)S(1)} %add_rsqrt_fusion), kind=kOutput, calls=%fused_computation.52 | convolution fusion | flops 2160590848 | bytes 10493952 | tf_op jit(solution)/shard_map/dot_general | solution.py:112
  35.1 1.3 copy.132
  36.4 78.3 %all-reduce.2.cloned.1.call-done = bf16[2048,512]{0,1:T(8,128)(2,1)} async-done(((bf16[2048,512]{0,1:T(8,128)(2,1)}), bf16[2048,512]{0,1:T(8,128)(2,1)}) %all-reduce.2.cloned.1.call-update) | async-done | bytes 2097168 | tf_op jit(solution)/shard_map/psum | solution.py:13
  114.7 2.7 fusion.58
  117.4 0.8 reshape.204
  118.2 1.7 copy.129
  119.9 143.6 %while.15 = (s32[]{:T(128)}, f32[4,2,512,128]{3,2,0,1:T(8,128)}, f32[4,2,512]{2,1,0:T(2,128)S(1)}, f32[4,2,512]{2,1,0:T(2,128)S(1)}, s32[4]{0:T(128)S(1)}, /*ind...) while((s32[]{:T(128)}, f32[4,2,512,128]{3,2,0,1:T(8,128)}, ...), condition=%wide.region_5.6_spmd.clone, body=%wide.region_2.5_spmd.clone.sunk | while | flops 1112539648 | bytes 102584528 | solution.py:147
  119.9 1.3 dynamic-slice_bitcast_fusion.2
  121.2 3.8 shift_right_arithmetic.114
  125.0 9.3 %shift_right_arithmetic.115 = s32[2,512,2048]{2,1,0:T(8,128)} reshape(s32[2,512,8,256]{3,2,1,0:T(8,128)} %shift_right_arithmetic.114) | data formatting | bytes 16777216 | tf_op jit(solution)/shard_map/while/body/eval_jaxpr/shift_right_arithmetic | solution.py:75
  136.1 6.6 %fusion.84 = (f32[2,512]{1,0:T(2,128)S(1)}, f32[2,512,2048]{2,1,0:T(8,128)}) fusion(pred[512,2048]{1,0:T(8,128)(4,1)S(1)} %broadcast_compare_fusion.3, bf16[2048,2,128]{2,0,1:T(8,128)(2,1)} %get-tuple-element.350, bf16[4,512,2,128]{3,1,2,0:T(8,128)(2,1)} %get-tuple-element.349, s32[]{:T(128)S(6)} %copy.189), kind=kOutput, calls=%fused_computation.26.clone.1 | convolution fusion | flops 543161344 | bytes 10752004 | tf_op jit(solution)/shard_map/while/body/eval_jaxpr/qhd,khd->hqk/dot_general | solution.py:131
  142.8 8.0 %fusion.85 = f32[4,2,512,128]{3,2,0,1:T(8,128)} fusion(f32[4,2,512,128]{3,2,0,1:T(8,128)} %get-tuple-element.332, s32[]{:T(128)S(6)} %copy.189, bf16[2048,2,128]{2,0,1:T(8,128)(2,1)} %get-tuple-element.352, s32[2,512,2048]{2,1,0:T(8,128)S(1)} %copy-done.2, f32[2,512,2048]{2,1,0:T(8,128)} %get-tuple-element.314, s32[2048]{0:T(1024)S(1)} %bitcast.169, ...), kind=kOutput, calls=%fused_computation.32.clone.1 | convolution fusion | flops 557842432 | bytes 19410948 | tf_op jit(solution)/shard_map/while/body/eval_jaxpr/hqk,khd->hqd/dot_general | solution.py:142
  150.8 5.0 fusion.86
  155.8 1.3 dynamic-slice_bitcast_fusion.2
  157.2 3.8 shift_right_arithmetic.114
  160.9 9.3 %shift_right_arithmetic.115 = s32[2,512,2048]{2,1,0:T(8,128)} reshape(s32[2,512,8,256]{3,2,1,0:T(8,128)} %shift_right_arithmetic.114) | data formatting | bytes 16777216 | tf_op jit(solution)/shard_map/while/body/eval_jaxpr/shift_right_arithmetic | solution.py:75
  172.0 6.6 %fusion.84 = (f32[2,512]{1,0:T(2,128)S(1)}, f32[2,512,2048]{2,1,0:T(8,128)}) fusion(pred[512,2048]{1,0:T(8,128)(4,1)S(1)} %broadcast_compare_fusion.3, bf16[2048,2,128]{2,0,1:T(8,128)(2,1)} %get-tuple-element.350, bf16[4,512,2,128]{3,1,2,0:T(8,128)(2,1)} %get-tuple-element.349, s32[]{:T(128)S(6)} %copy.189), kind=kOutput, calls=%fused_computation.26.clone.1 | convolution fusion | flops 543161344 | bytes 10752004 | tf_op jit(solution)/shard_map/while/body/eval_jaxpr/qhd,khd->hqk/dot_general | solution.py:131
  178.7 8.0 %fusion.85 = f32[4,2,512,128]{3,2,0,1:T(8,128)} fusion(f32[4,2,512,128]{3,2,0,1:T(8,128)} %get-tuple-element.332, s32[]{:T(128)S(6)} %copy.189, bf16[2048,2,128]{2,0,1:T(8,128)(2,1)} %get-tuple-element.352, s32[2,512,2048]{2,1,0:T(8,128)S(1)} %copy-done.2, f32[2,512,2048]{2,1,0:T(8,128)} %get-tuple-element.314, s32[2048]{0:T(1024)S(1)} %bitcast.169, ...), kind=kOutput, calls=%fused_computation.32.clone.1 | convolution fusion | flops 557842432 | bytes 19410948 | tf_op jit(solution)/shard_map/while/body/eval_jaxpr/hqk,khd->hqd/dot_general | solution.py:142
  186.7 5.0 fusion.86
  191.8 1.3 dynamic-slice_bitcast_fusion.2
  193.1 3.8 shift_right_arithmetic.114
  196.9 9.3 %shift_right_arithmetic.115 = s32[2,512,2048]{2,1,0:T(8,128)} reshape(s32[2,512,8,256]{3,2,1,0:T(8,128)} %shift_right_arithmetic.114) | data formatting | bytes 16777216 | tf_op jit(solution)/shard_map/while/body/eval_jaxpr/shift_right_arithmetic | solution.py:75
  208.0 6.6 %fusion.84 = (f32[2,512]{1,0:T(2,128)S(1)}, f32[2,512,2048]{2,1,0:T(8,128)}) fusion(pred[512,2048]{1,0:T(8,128)(4,1)S(1)} %broadcast_compare_fusion.3, bf16[2048,2,128]{2,0,1:T(8,128)(2,1)} %get-tuple-element.350, bf16[4,512,2,128]{3,1,2,0:T(8,128)(2,1)} %get-tuple-element.349, s32[]{:T(128)S(6)} %copy.189), kind=kOutput, calls=%fused_computation.26.clone.1 | convolution fusion | flops 543161344 | bytes 10752004 | tf_op jit(solution)/shard_map/while/body/eval_jaxpr/qhd,khd->hqk/dot_general | solution.py:131
  214.6 8.0 %fusion.85 = f32[4,2,512,128]{3,2,0,1:T(8,128)} fusion(f32[4,2,512,128]{3,2,0,1:T(8,128)} %get-tuple-element.332, s32[]{:T(128)S(6)} %copy.189, bf16[2048,2,128]{2,0,1:T(8,128)(2,1)} %get-tuple-element.352, s32[2,512,2048]{2,1,0:T(8,128)S(1)} %copy-done.2, f32[2,512,2048]{2,1,0:T(8,128)} %get-tuple-element.314, s32[2048]{0:T(1024)S(1)} %bitcast.169, ...), kind=kOutput, calls=%fused_computation.32.clone.1 | convolution fusion | flops 557842432 | bytes 19410948 | tf_op jit(solution)/shard_map/while/body/eval_jaxpr/hqk,khd->hqd/dot_general | solution.py:142
  222.6 5.0 fusion.86
  227.7 1.3 dynamic-slice_bitcast_fusion.2
  229.0 3.8 shift_right_arithmetic.114
  232.8 9.3 %shift_right_arithmetic.115 = s32[2,512,2048]{2,1,0:T(8,128)} reshape(s32[2,512,8,256]{3,2,1,0:T(8,128)} %shift_right_arithmetic.114) | data formatting | bytes 16777216 | tf_op jit(solution)/shard_map/while/body/eval_jaxpr/shift_right_arithmetic | solution.py:75
  243.9 6.6 %fusion.84 = (f32[2,512]{1,0:T(2,128)S(1)}, f32[2,512,2048]{2,1,0:T(8,128)}) fusion(pred[512,2048]{1,0:T(8,128)(4,1)S(1)} %broadcast_compare_fusion.3, bf16[2048,2,128]{2,0,1:T(8,128)(2,1)} %get-tuple-element.350, bf16[4,512,2,128]{3,1,2,0:T(8,128)(2,1)} %get-tuple-element.349, s32[]{:T(128)S(6)} %copy.189), kind=kOutput, calls=%fused_computation.26.clone.1 | convolution fusion | flops 543161344 | bytes 10752004 | tf_op jit(solution)/shard_map/while/body/eval_jaxpr/qhd,khd->hqk/dot_general | solution.py:131
  250.5 8.0 %fusion.85 = f32[4,2,512,128]{3,2,0,1:T(8,128)} fusion(f32[4,2,512,128]{3,2,0,1:T(8,128)} %get-tuple-element.332, s32[]{:T(128)S(6)} %copy.189, bf16[2048,2,128]{2,0,1:T(8,128)(2,1)} %get-tuple-element.352, s32[2,512,2048]{2,1,0:T(8,128)S(1)} %copy-done.2, f32[2,512,2048]{2,1,0:T(8,128)} %get-tuple-element.314, s32[2048]{0:T(1024)S(1)} %bitcast.169, ...), kind=kOutput, calls=%fused_computation.32.clone.1 | convolution fusion | flops 557842432 | bytes 19410948 | tf_op jit(solution)/shard_map/while/body/eval_jaxpr/hqk,khd->hqd/dot_general | solution.py:142
  258.6 5.0 fusion.86
  263.7 11.5 %all_to_all.26 = f32[16,2,2048]{2,1,0:T(2,128)S(1)} all-to-all(f32[16,2,2048]{2,1,0:T(2,128)S(1)} %broadcast_in_dim.109), channel_id=1, replica_groups=mesh['seq'=16,'head'=8] {'seq'}, dimensions={0} | all-to-all | bytes 524288 | tf_op jit(solution)/shard_map/all_to_all | solution.py:18
  275.9 2.0 fusion.33
  277.9 1.8 pad_maximum_fusion
  279.7 74.6 %reduce-scatter.2.cloned.1.call-done = bf16[2,128,129]{2,1,0:T(8,128)(2,1)} async-done(((bf16[2,2048,129]{2,1,0:T(8,128)(2,1)}), bf16[2,128,129]{2,1,0:T(8,128)(2,1)}) %reduce-scatter.2.cloned.1.call-update) | async-done | bytes 66064 | tf_op jit(solution)/shard_map/reduce_scatter | solution.py:33
  354.4 0.9 convert_reduce_fusion.2
  355.3 1.0 fusion.47
  356.8 0.8 copy.178
  357.6 6.6 %all-to-all-start.1 = ((bf16[8,128,256]{2,1,0:T(8,128)(2,1)}), bf16[8,128,256]{2,1,0:T(8,128)(2,1)S(1)}, u32[]{:S(2)}, u32[]{:S(2)}) async-start(bf16[8,128,256]{2,1,0:T(8,128)(2,1)} %bitcast.136), calls=%async_computation.2 | async-start | bytes 1048576 | tf_op jit(solution)/shard_map/all_to_all | solution.py:47
  364.2 1.1 constant_dynamic-slice_fusion
  365.8 7.7 %all-to-all-done.1 = bf16[8,128,256]{2,1,0:T(8,128)(2,1)S(1)} async-done(((bf16[8,128,256]{2,1,0:T(8,128)(2,1)}), bf16[8,128,256]{2,1,0:T(8,128)(2,1)S(1)}, u32[]{:S(2)}, u32[]{:S(2)}) %all-to-all-start.1) | async-done | bytes 524320 | tf_op jit(solution)/shard_map/all_to_all | solution.py:47
  373.7 0.9 fusion.38
  374.6 7.9 %all_to_all.27 = f32[8,1,128]{2,1,0:T(1,128)S(1)} all-to-all(f32[8,1,128]{2,1,0:T(1,128)S(1)} %broadcast_in_dim.110), channel_id=1, replica_groups=mesh['seq'=16,'head'=8] {'head'}, dimensions={0} | all-to-all | bytes 8192 | tf_op jit(solution)/shard_map/all_to_all | solution.py:18
  382.7 12.4 %all_to_all.28 = bf16[8,128,256]{1,2,0:T(8,128)(2,1)S(1)} all-to-all(bf16[8,128,256]{1,2,0:T(8,128)(2,1)S(1)} %broadcast_in_dim.111), channel_id=1, replica_groups=mesh['seq'=16,'head'=8] {'head'}, dimensions={0} | all-to-all | bytes 1048576 | tf_op jit(solution)/shard_map/all_to_all | solution.py:18
  397.9 1.6 fusion.35
  399.6 1.6 convolution_convert_fusion.7
  401.2 36.8 %all-gather.2.cloned.1.call-done = bf16[2048,512]{1,0:T(8,128)(2,1)} async-done(((bf16[128,512]{1,0:T(8,128)(2,1)}), bf16[2048,512]{1,0:T(8,128)(2,1)}) %all-gather.2.cloned.1.call-update) | async-done | bytes 2097168 | tf_op jit(solution)/shard_map/all_gather | solution.py:69
  437.9 37.6 %conditional.1 = (f32[2,128]{1,0:T(2,128)S(1)}, f32[2,128,128]{1,2,0:T(8,128)}) conditional(s32[]{:T(128)} %convert_element_type.124, () %tuple.18, (s32[2048]{0:T(1024)S(1)}, s32[128]{0:T(128)S(1)}, bf16[128,256]{1,0:T(8,128)(2,1)S(1)}, bf16[2048,512]{1,0:T(8,128)(2,1)}, s32[2048]{0:T(1024)S(1)}, /*index=5*/s32[2048]{0:T(1024)S(1)}, ...), branch_computations={%region_12.13_spmd, %region_13.16_spmd} | conditional | flops 275009280 | bytes 45337160 | solution.py:238
  437.9 2.9 copy.142
  440.9 1.2 fusion.56
  443.6 8.6 %copy.143 = f32[2,128,2048]{1,0,2:T(2,128)} copy(f32[2,128,2048]{1,2,0:T(8,128)S(1)} %copy-done.3) | data formatting | bytes 4194304 | tf_op jit(solution)/shard_map
  452.2 16.1 %gather_fusion = f32[2048,2,128]{2,1,0:T(2,128)} fusion(f32[2,128,2048]{1,0,2:T(2,128)} %copy.143, s32[2048]{0:T(1024)S(1)} %fusion.12), kind=kCustom, calls=%fused_computation | custom fusion | bytes 4202496 | tf_op jit(solution)/shard_map/cond/branch_1_fun/jit(_take)/gather | solution.py:227
  468.2 4.2 copy.125
  472.4 3.1 fusion.6
  475.5 1.0 divide_convert_fusion
  476.5 1.6 convolution_convert_fusion.3
  478.1 15.6 %all_to_all.29 = bf16[8,128,256]{2,1,0:T(8,128)(2,1)S(1)} all-to-all(bf16[8,128,256]{2,1,0:T(8,128)(2,1)S(1)} %bitcast.163), channel_id=1, replica_groups=mesh['seq'=16,'head'=8] {'head'}, dimensions={0} | all-to-all | bytes 1048576 | tf_op jit(solution)/shard_map/all_to_all | solution.py:47
  494.0 0.7 copy.148
  (104 shorter events, 11.7 us)
Async XLA Ops:
  6.5 7.1 %copy-start = (bf16[2048,256]{1,0:T(8,128)(2,1)S(1)}, bf16[2048,256]{1,0:T(8,128)(2,1)}, u32[]{:S(2)}) copy-start(bf16[2048,256]{1,0:T(8,128)(2,1)} %param.17) | copy-start | bytes 3145732
  6.5 108.2 %all-reduce.2.cloned.1.call-start = ((), (), s32[]{:S(2)}) async-start(), calls=%async_computation.6 | async-start | bytes 4194304 | tf_op jit(solution)/shard_map/psum | solution.py:13
  21.4 333.0 %reduce-scatter.2.cloned.1.call-start = ((), (), s32[]{:S(2)}) async-start(), calls=%async_computation.7 | async-start | bytes 2228224 | tf_op jit(solution)/shard_map/reduce_scatter | solution.py:33
  21.6 7.6 %copy-start.10 = (bf16[2048,256]{1,0:T(8,128)(2,1)S(1)}, bf16[2048,256]{1,0:T(8,128)(2,1)}, u32[]{:S(2)}) copy-start(bf16[2048,256]{1,0:T(8,128)(2,1)} %param.19) | copy-start | bytes 3145732
  136.1 6.7 %copy-start.2 = (s32[2,512,2048]{2,1,0:T(8,128)S(1)}, s32[2,512,2048]{2,1,0:T(8,128)}, u32[]{:S(2)}) copy-start(s32[2,512,2048]{2,1,0:T(8,128)} %shift_right_arithmetic.115) | copy-start | bytes 25165828 | tf_op jit(solution)/shard_map/while
  172.0 6.7 %copy-start.2 = (s32[2,512,2048]{2,1,0:T(8,128)S(1)}, s32[2,512,2048]{2,1,0:T(8,128)}, u32[]{:S(2)}) copy-start(s32[2,512,2048]{2,1,0:T(8,128)} %shift_right_arithmetic.115) | copy-start | bytes 25165828 | tf_op jit(solution)/shard_map/while
  207.9 6.7 %copy-start.2 = (s32[2,512,2048]{2,1,0:T(8,128)S(1)}, s32[2,512,2048]{2,1,0:T(8,128)}, u32[]{:S(2)}) copy-start(s32[2,512,2048]{2,1,0:T(8,128)} %shift_right_arithmetic.115) | copy-start | bytes 25165828 | tf_op jit(solution)/shard_map/while
  243.9 6.7 %copy-start.2 = (s32[2,512,2048]{2,1,0:T(8,128)S(1)}, s32[2,512,2048]{2,1,0:T(8,128)}, u32[]{:S(2)}) copy-start(s32[2,512,2048]{2,1,0:T(8,128)} %shift_right_arithmetic.115) | copy-start | bytes 25165828 | tf_op jit(solution)/shard_map/while
  275.9 80.5 %copy-start.6 = (bf16[256,2048]{1,0:T(8,128)(2,1)S(1)}, bf16[256,2048]{1,0:T(8,128)(2,1)}, u32[]{:S(2)}) copy-start(bf16[256,2048]{1,0:T(8,128)(2,1)} %param.20) | copy-start | bytes 3145732
  356.7 38.3 %copy-start.7 = (bf16[2048,256]{1,0:T(8,128)(2,1)S(1)}, bf16[2048,256]{1,0:T(8,128)(2,1)}, u32[]{:S(2)}) copy-start(bf16[2048,256]{1,0:T(8,128)(2,1)} %param.23) | copy-start | bytes 3145732
  357.6 15.9 %all-to-all-start.1 = ((bf16[8,128,256]{2,1,0:T(8,128)(2,1)}), bf16[8,128,256]{2,1,0:T(8,128)(2,1)S(1)}, u32[]{:S(2)}, u32[]{:S(2)}) async-start(bf16[8,128,256]{2,1,0:T(8,128)(2,1)} %bitcast.136), calls=%async_computation.2 | async-start | bytes 1048576 | tf_op jit(solution)/shard_map/all_to_all | solution.py:47
  364.2 31.3 %copy-start.8 = (bf16[2048,256]{1,0:T(8,128)(2,1)S(1)}, bf16[2048,256]{1,0:T(8,128)(2,1)}, u32[]{:S(2)}) copy-start(bf16[2048,256]{1,0:T(8,128)(2,1)} %param.22) | copy-start | bytes 3145732
  364.2 73.8 %all-gather.2.cloned.1.call-start = ((), (), s32[]{:S(2)}) async-start(), calls=%async_computation.8 | async-start | bytes 2228224 | tf_op jit(solution)/shard_map/all_gather | solution.py:69
  365.8 16.7 %copy-start.4 = (f32[2,128,256]{1,2,0:T(8,128)}, f32[2,128,256]{1,2,0:T(8,128)S(1)}, u32[]{:S(2)}) copy-start(f32[2,128,256]{1,2,0:T(8,128)S(1)} %fusion.37) | copy-start | bytes 786436
  440.9 2.7 copy-start.3
  452.2 20.2 %copy-start.9 = (bf16[2048,256]{0,1:T(8,128)(2,1)S(1)}, bf16[2048,256]{0,1:T(8,128)(2,1)}, u32[]{:S(2)}) copy-start(bf16[2048,256]{0,1:T(8,128)(2,1)} %get-tuple-element.237) | copy-start | bytes 3145732 | tf_op jit(solution)/shard_map/cond
  475.5 18.4 %copy-start.5 = (f32[2,128,256]{1,2,0:T(8,128)S(1)}, f32[2,128,256]{1,2,0:T(8,128)}, u32[]{:S(2)}) copy-start(f32[2,128,256]{1,2,0:T(8,128)} %copy-done.4) | copy-start | bytes 786436
  475.5 19.2 %copy-start.1 = (bf16[2048,256]{1,0:T(8,128)(2,1)S(1)}, bf16[2048,256]{1,0:T(8,128)(2,1)}, u32[]{:S(2)}) copy-start(bf16[2048,256]{1,0:T(8,128)(2,1)} %param.17) | copy-start | bytes 3145732
Sparse Core Ops, SparseCore 0:
  21.5 93.1 all-reduce.1
  279.8 74.4 reduce-scatter.1
  396.7 41.2 all-gather.1
where the time goes:
time: 503 us; the launch traced here: 501 us
  waiting for transfers between devices  197 us (39%)
  local copies, waits for them, and re-layouts  107 us (21%)
  matrix products  84.7 us (17%)
  blocking collectives  47.5 us (9%)
  other arithmetic  41.3 us (8%)
  between operations  14.1 us (3%)
  starting transfers between devices  6.82 us (1%)
    psum x1, waiting for transfers between devices, from_root(): return lax.psum(kept, axis)  78.3 us
    reduce_scatter x1, waiting for transfers between devices, side_by_side(): filled = lax.psum_scatter(both, axis, scatter_dimension=dim, tiled=True)  74.6 us
    shift_right_arithmetic x14, local copies, waits for them, and re-layouts, unpack_bits(): jnp.right_shift(packed_words[..., None, :], shifts[:, None])  57.7 us
    all_gather x1, waiting for transfers between devices, side_by_side_2(): filled = lax.all_gather(both, axis, axis=dim, tiled=True)  36.8 us
    dot_general x4, matrix products, cross_block(): jnp.einsum('hqk,khd->hqd', weights, value_heads, preferred_element_type=j...  32.1 us
    all_to_all x3, blocking collectives, copy_for_each(): lax.all_to_all(jnp.broadcast_to(value[None], (size, *value.shape)), axis,...  31.9 us
    dot_general x4, matrix products, cross_block(): jnp.einsum('qhd,khd->hqk', query_block, key_heads, preferred_element_type...  26.5 us
    gather x2, local copies, waits for them, and re-layouts, update(): keep_flags = jnp.take(latent_mask, key_index, axis=2)  20.2 us
  transfers between devices with their start and end apart: 4, of which 4 were waited for; matrix products, arithmetic and copies ran while one was open for 4% of the time, Pallas kernels for 0%

commit v1 on v0

--- a/solution.py
+++ b/solution.py
@@ -10,7 +10,7 @@
 
 def from_root(value, axis, source):
     kept = jnp.where(lax.axis_index(axis) == source, value, 0).astype(value.dtype)
-    return lax.psum(kept, axis)
+    return jnp.sum(lax.all_gather(kept, axis), axis=0)
 
 
 def copy_for_each(value, axis):

time: 503 us -> 601 us (1.19)
  waiting for transfers between devices: 197 us -> 302 us
  matrix products: 84.7 us -> 73.6 us
    all_gather x0 -> x1, waiting for transfers between devices: none -> 185 us  [from_root(): return jnp.sum(lax.all_gather(kept, axis), axis=0)]
    psum x1 -> x0, waiting for transfers between devices: 78.3 us -> none  [from_root(): return lax.psum(kept, axis)]
    dot_general x4, matrix products: 26.5 us -> 13.2 us  [cross_block(): jnp.einsum('qhd,khd->hqk', query_block, key_heads, preferred_element_type...]
    reduce_sum x0 -> x1, other arithmetic: none -> 11.6 us  [from_root(): return jnp.sum(lax.all_gather(kept, axis), axis=0)]
    reduce_sum x4, other arithmetic: 20 us -> 11.3 us  [cross_block(): row_sum = jnp.sum(exponent, axis=-1)]
where the time goes in v1:
time: 601 us; the launch traced here: 599 us
  waiting for transfers between devices  302 us (50%)
  local copies, waits for them, and re-layouts  110 us (18%)
  matrix products  73.6 us (12%)
  blocking collectives  48.3 us (8%)
  other arithmetic  42.1 us (7%)
  between operations  14.1 us (2%)
  starting transfers between devices  6.76 us (1%)
    all_gather x1, waiting for transfers between devices, from_root(): return jnp.sum(lax.all_gather(kept, axis), axis=0)  185 us
    reduce_scatter x1, waiting for transfers between devices, side_by_side(): filled = lax.psum_scatter(both, axis, scatter_dimension=dim, tiled=True)  72.9 us
    shift_right_arithmetic x14, local copies, waits for them, and re-layouts, unpack_bits(): jnp.right_shift(packed_words[..., None, :], shifts[:, None])  57.9 us
    all_gather x1, waiting for transfers between devices, side_by_side_2(): filled = lax.all_gather(both, axis, axis=dim, tiled=True)  36.8 us
    dot_general x4, matrix products, cross_block(): jnp.einsum('hqk,khd->hqd', weights, value_heads, preferred_element_type=j...  34.2 us
    all_to_all x3, blocking collectives, copy_for_each(): lax.all_to_all(jnp.broadcast_to(value[None], (size, *value.shape)), axis,...  32.7 us
    gather x2, local copies, waits for them, and re-layouts, update(): keep_flags = jnp.take(latent_mask, key_index, axis=2)  20.2 us
    all_to_all x1, blocking collectives, sum_at_owner(): lax.all_to_all(parts, axis, split_axis=0, concat_axis=0, tiled=True)  15.6 us
  transfers between devices with their start and end apart: 4, of which 4 were waited for; matrix products, arithmetic and copies ran while one was open for 4% of the time, Pallas kernels for 0%

profile of v1, /device:TPU:1, one launch (start us, length us, event | category | flops | bytes accessed | tf_op | source)
XLA Modules:
  0.0 599.3 jit_solution(17042551040777457872)
XLA Ops:
  6.5 5.2 fusion.28
  11.7 1.3 constant_dynamic-slice_fusion.4
  13.0 1.4 copy.144
  14.5 6.0 fusion.30
  20.9 2.5 copy.145
  23.6 6.2 %convolution_convert_fusion.1 = bf16[2048,256]{0,1:T(8,128)(2,1)S(1)} fusion(bf16[2048,256]{1,0:T(8,128)(2,1)} %param.18, bf16[2048,2048]{1,0:T(8,128)(2,1)} %param.16, f32[2048]{0:T(1024)S(1)} %add_rsqrt_fusion), kind=kOutput, calls=%fused_computation.52 | convolution fusion | flops 2160590848 | bytes 10493952 | tf_op jit(solution)/shard_map/dot_general | solution.py:111
  29.8 1.5 copy.149
  31.3 5.9 convolution_convert_fusion
  37.2 1.3 copy.151
  38.5 185.3 %all-gather.3.cloned.1.call-done = bf16[16,2048,512]{2,1,0:T(8,128)(2,1)} async-done(((bf16[1,2048,512]{2,1,0:T(8,128)(2,1)}), bf16[16,2048,512]{2,1,0:T(8,128)(2,1)}) %all-gather.3.cloned.1.call-update) | async-done | bytes 33554448 | tf_op jit(solution)/shard_map/all_gather | solution.py:13
  223.8 11.6 %reduce_sum.76 = bf16[2048,512]{1,0:T(8,128)(2,1)S(1)} reduce(bf16[16,2048,512]{2,1,0:T(8,128)(2,1)} %all-gather.3.cloned.1.call-done, bf16[]{:T(256)} %constant.99.clone.1), dimensions={0}, to_apply=%region_1.2 | reduce | flops 15728640 | bytes 35651584 | tf_op jit(solution)/shard_map/reduce_sum | solution.py:13
  235.4 1.2 fusion.56
  236.9 126.4 %while.15 = (s32[]{:T(128)}, f32[4,2,512,128]{3,2,0,1:T(8,128)}, f32[4,2,512]{2,1,0:T(2,128)S(1)}, f32[4,2,512]{2,1,0:T(2,128)S(1)}, s32[4]{0:T(128)S(1)}, /*ind...) while((s32[]{:T(128)}, f32[4,2,512,128]{3,2,0,1:T(8,128)}, ...), condition=%wide.region_5.6_spmd.clone, body=%wide.region_2.5_spmd.clone.sunk | while | flops 1112539648 | bytes 107303664 | solution.py:147
  239.0 3.3 fusion.82
  242.3 2.8 fusion.84
  245.5 1.3 dynamic-slice_bitcast_fusion.2
  246.8 3.8 shift_right_arithmetic.114
  250.6 9.4 %shift_right_arithmetic.115 = s32[2,512,2048]{2,1,0:T(8,128)} reshape(s32[2,512,8,256]{3,2,1,0:T(8,128)} %shift_right_arithmetic.114) | data formatting | bytes 16777216 | tf_op jit(solution)/shard_map/while/body/eval_jaxpr/shift_right_arithmetic | solution.py:75
  260.0 8.5 %fusion.83 = f32[4,2,512,128]{3,2,0,1:T(8,128)} fusion(f32[4,2,512,128]{3,2,0,1:T(8,128)} %get-tuple-element.342, s32[]{:T(128)} %get-tuple-element.341, bf16[2048,2,128]{2,0,1:T(8,128)(2,1)S(1)} %copy-done.10, s32[2,512,2048]{2,1,0:T(8,128)} %shift_right_arithmetic.115, f32[2,512,2048]{2,1,0:T(8,128)} %copy-done.2, s32[2048]{0:T(1024)S(1)} %bitcast.171, ...), kind=kOutput, calls=%fused_computation.32.clone.1 | convolution fusion | flops 557842432 | bytes 19411456 | tf_op jit(solution)/shard_map/while/body/eval_jaxpr/hqk,khd->hqd/dot_general | solution.py:142
  270.6 3.3 fusion.82
  273.9 2.8 fusion.84
  277.1 1.3 dynamic-slice_bitcast_fusion.2
  278.4 3.8 shift_right_arithmetic.114
  282.2 9.4 %shift_right_arithmetic.115 = s32[2,512,2048]{2,1,0:T(8,128)} reshape(s32[2,512,8,256]{3,2,1,0:T(8,128)} %shift_right_arithmetic.114) | data formatting | bytes 16777216 | tf_op jit(solution)/shard_map/while/body/eval_jaxpr/shift_right_arithmetic | solution.py:75
  291.6 8.6 %fusion.83 = f32[4,2,512,128]{3,2,0,1:T(8,128)} fusion(f32[4,2,512,128]{3,2,0,1:T(8,128)} %get-tuple-element.342, s32[]{:T(128)} %get-tuple-element.341, bf16[2048,2,128]{2,0,1:T(8,128)(2,1)S(1)} %copy-done.10, s32[2,512,2048]{2,1,0:T(8,128)} %shift_right_arithmetic.115, f32[2,512,2048]{2,1,0:T(8,128)} %copy-done.2, s32[2048]{0:T(1024)S(1)} %bitcast.171, ...), kind=kOutput, calls=%fused_computation.32.clone.1 | convolution fusion | flops 557842432 | bytes 19411456 | tf_op jit(solution)/shard_map/while/body/eval_jaxpr/hqk,khd->hqd/dot_general | solution.py:142
  302.2 3.3 fusion.82
  305.5 2.8 fusion.84
  308.7 1.3 dynamic-slice_bitcast_fusion.2
  310.0 3.8 shift_right_arithmetic.114
  313.8 9.4 %shift_right_arithmetic.115 = s32[2,512,2048]{2,1,0:T(8,128)} reshape(s32[2,512,8,256]{3,2,1,0:T(8,128)} %shift_right_arithmetic.114) | data formatting | bytes 16777216 | tf_op jit(solution)/shard_map/while/body/eval_jaxpr/shift_right_arithmetic | solution.py:75
  323.2 8.5 %fusion.83 = f32[4,2,512,128]{3,2,0,1:T(8,128)} fusion(f32[4,2,512,128]{3,2,0,1:T(8,128)} %get-tuple-element.342, s32[]{:T(128)} %get-tuple-element.341, bf16[2048,2,128]{2,0,1:T(8,128)(2,1)S(1)} %copy-done.10, s32[2,512,2048]{2,1,0:T(8,128)} %shift_right_arithmetic.115, f32[2,512,2048]{2,1,0:T(8,128)} %copy-done.2, s32[2048]{0:T(1024)S(1)} %bitcast.171, ...), kind=kOutput, calls=%fused_computation.32.clone.1 | convolution fusion | flops 557842432 | bytes 19411456 | tf_op jit(solution)/shard_map/while/body/eval_jaxpr/hqk,khd->hqd/dot_general | solution.py:142
  333.8 3.3 fusion.82
  337.1 2.8 fusion.84
  340.3 1.3 dynamic-slice_bitcast_fusion.2
  341.6 3.8 shift_right_arithmetic.114
  345.4 9.4 %shift_right_arithmetic.115 = s32[2,512,2048]{2,1,0:T(8,128)} reshape(s32[2,512,8,256]{3,2,1,0:T(8,128)} %shift_right_arithmetic.114) | data formatting | bytes 16777216 | tf_op jit(solution)/shard_map/while/body/eval_jaxpr/shift_right_arithmetic | solution.py:75
  354.8 8.6 %fusion.83 = f32[4,2,512,128]{3,2,0,1:T(8,128)} fusion(f32[4,2,512,128]{3,2,0,1:T(8,128)} %get-tuple-element.342, s32[]{:T(128)} %get-tuple-element.341, bf16[2048,2,128]{2,0,1:T(8,128)(2,1)S(1)} %copy-done.10, s32[2,512,2048]{2,1,0:T(8,128)} %shift_right_arithmetic.115, f32[2,512,2048]{2,1,0:T(8,128)} %copy-done.2, s32[2048]{0:T(1024)S(1)} %bitcast.171, ...), kind=kOutput, calls=%fused_computation.32.clone.1 | convolution fusion | flops 557842432 | bytes 19411456 | tf_op jit(solution)/shard_map/while/body/eval_jaxpr/hqk,khd->hqd/dot_general | solution.py:142
  363.5 12.3 %all_to_all.26 = f32[16,2,2048]{2,1,0:T(2,128)S(1)} all-to-all(f32[16,2,2048]{2,1,0:T(2,128)S(1)} %broadcast_in_dim.109), channel_id=1, replica_groups=mesh['seq'=16,'head'=8] {'seq'}, dimensions={0} | all-to-all | bytes 524288 | tf_op jit(solution)/shard_map/all_to_all | solution.py:18
  376.5 2.0 fusion.31
  378.5 1.8 pad_maximum_fusion
  380.3 72.9 %reduce-scatter.2.cloned.1.call-done = bf16[2,128,129]{2,1,0:T(8,128)(2,1)} async-done(((bf16[2,2048,129]{2,1,0:T(8,128)(2,1)}), bf16[2,128,129]{2,1,0:T(8,128)(2,1)}) %reduce-scatter.2.cloned.1.call-update) | async-done | bytes 66064 | tf_op jit(solution)/shard_map/reduce_scatter | solution.py:33
  453.1 0.9 convert_reduce_fusion.2
  454.1 1.0 fusion.45
  455.5 0.8 copy.203
  456.3 6.7 %all-to-all-start.1 = ((bf16[8,128,256]{2,1,0:T(8,128)(2,1)}), bf16[8,128,256]{2,1,0:T(8,128)(2,1)S(1)}, u32[]{:S(2)}, u32[]{:S(2)}) async-start(bf16[8,128,256]{2,1,0:T(8,128)(2,1)} %bitcast.137), calls=%async_computation.2 | async-start | bytes 1048576 | tf_op jit(solution)/shard_map/all_to_all | solution.py:47
  463.1 1.1 constant_dynamic-slice_fusion.1
  464.7 0.9 constant_dynamic-slice_fusion.3
  465.7 6.7 %all-to-all-done.1 = bf16[8,128,256]{2,1,0:T(8,128)(2,1)S(1)} async-done(((bf16[8,128,256]{2,1,0:T(8,128)(2,1)}), bf16[8,128,256]{2,1,0:T(8,128)(2,1)S(1)}, u32[]{:S(2)}, u32[]{:S(2)}) %all-to-all-start.1) | async-done | bytes 524320 | tf_op jit(solution)/shard_map/all_to_all | solution.py:47
  472.6 7.9 %all_to_all.27 = f32[8,1,128]{2,1,0:T(1,128)S(1)} all-to-all(f32[8,1,128]{2,1,0:T(1,128)S(1)} %broadcast_in_dim.110), channel_id=1, replica_groups=mesh['seq'=16,'head'=8] {'head'}, dimensions={0} | all-to-all | bytes 8192 | tf_op jit(solution)/shard_map/all_to_all | solution.py:18
  480.7 12.4 %all_to_all.28 = bf16[8,128,256]{1,2,0:T(8,128)(2,1)S(1)} all-to-all(bf16[8,128,256]{1,2,0:T(8,128)(2,1)S(1)} %broadcast_in_dim.111), channel_id=1, replica_groups=mesh['seq'=16,'head'=8] {'head'}, dimensions={0} | all-to-all | bytes 1048576 | tf_op jit(solution)/shard_map/all_to_all | solution.py:18
  495.3 1.6 fusion.33
  497.6 1.6 convolution_convert_fusion.7
  499.2 36.8 %all-gather.5.cloned.1.call-done = bf16[2048,512]{1,0:T(8,128)(2,1)} async-done(((bf16[128,512]{1,0:T(8,128)(2,1)}), bf16[2048,512]{1,0:T(8,128)(2,1)}) %all-gather.5.cloned.1.call-update) | async-done | bytes 2097168 | tf_op jit(solution)/shard_map/all_gather | solution.py:69
  536.0 37.6 %conditional.1 = (f32[2,128]{1,0:T(2,128)S(1)}, f32[2,128,128]{1,2,0:T(8,128)}) conditional(s32[]{:T(128)} %convert_element_type.126, () %tuple.18, (s32[2048]{0:T(1024)S(1)}, s32[128]{0:T(128)S(1)}, bf16[128,256]{1,0:T(8,128)(2,1)S(1)}, bf16[2048,512]{1,0:T(8,128)(2,1)}, s32[2048]{0:T(1024)S(1)}, /*index=5*/s32[2048]{0:T(1024)S(1)}, ...), branch_computations={%region_12.13_spmd, %region_13.16_spmd} | conditional | flops 275009280 | bytes 45337160 | solution.py:238
  536.2 2.9 copy.160
  539.2 1.2 fusion.54
  541.1 8.6 %copy.161 = f32[2,128,2048]{1,0,2:T(2,128)} copy(f32[2,128,2048]{1,2,0:T(8,128)S(1)} %copy-done.3) | data formatting | bytes 4194304 | tf_op jit(solution)/shard_map
  549.7 16.1 %gather_fusion = f32[2048,2,128]{2,1,0:T(2,128)} fusion(f32[2,128,2048]{1,0,2:T(2,128)} %copy.161, s32[2048]{0:T(1024)S(1)} %fusion.12), kind=kCustom, calls=%fused_computation | custom fusion | bytes 4202496 | tf_op jit(solution)/shard_map/cond/branch_1_fun/jit(_take)/gather | solution.py:227
  565.7 4.2 copy.142
  569.9 3.1 fusion.6
  573.6 1.0 divide_convert_fusion
  574.6 1.6 convolution_convert_fusion.3
  576.2 15.6 %all_to_all.29 = bf16[8,128,256]{2,1,0:T(8,128)(2,1)S(1)} all-to-all(bf16[8,128,256]{2,1,0:T(8,128)(2,1)S(1)} %bitcast.165), channel_id=1, replica_groups=mesh['seq'=16,'head'=8] {'head'}, dimensions={0} | all-to-all | bytes 1048576 | tf_op jit(solution)/shard_map/all_to_all | solution.py:47
  592.1 0.7 copy.165
  (121 shorter events, 14.3 us)
Async XLA Ops:
  6.5 7.9 %copy-start = (bf16[2048,256]{1,0:T(8,128)(2,1)S(1)}, bf16[2048,256]{1,0:T(8,128)(2,1)}, u32[]{:S(2)}) copy-start(bf16[2048,256]{1,0:T(8,128)(2,1)} %param.17) | copy-start | bytes 3145732
  6.5 217.2 %all-gather.3.cloned.1.call-start = ((), (), s32[]{:S(2)}) async-start(), calls=%async_computation.6 | async-start | bytes 35651584 | tf_op jit(solution)/shard_map/all_gather | solution.py:13
  14.5 6.0 %copy-start.4 = (bf16[2048,256]{0,1:T(8,128)(2,1)S(1)}, bf16[2048,256]{0,1:T(8,128)(2,1)}, u32[]{:S(2)}) copy-start(bf16[2048,256]{0,1:T(8,128)(2,1)} %copy.144) | copy-start | bytes 3145732
  23.5 429.7 %reduce-scatter.2.cloned.1.call-start = ((), (), s32[]{:S(2)}) async-start(), calls=%async_computation.7 | async-start | bytes 2228224 | tf_op jit(solution)/shard_map/reduce_scatter | solution.py:33
  23.5 7.7 %copy-start.12 = (bf16[2048,256]{1,0:T(8,128)(2,1)S(1)}, bf16[2048,256]{1,0:T(8,128)(2,1)}, u32[]{:S(2)}) copy-start(bf16[2048,256]{1,0:T(8,128)(2,1)} %param.19) | copy-start | bytes 3145732
  242.3 3.2 copy-start.2
  250.6 9.4 %copy-start.10 = (bf16[2048,2,128]{2,0,1:T(8,128)(2,1)S(1)}, bf16[2048,2,128]{2,0,1:T(8,128)(2,1)}, u32[]{:S(2)}) copy-start(bf16[2048,2,128]{2,0,1:T(8,128)(2,1)} %get-tuple-element.362) | copy-start | bytes 3145732 | tf_op jit(solution)/shard_map/while
  273.9 3.2 copy-start.2
  282.2 9.4 %copy-start.10 = (bf16[2048,2,128]{2,0,1:T(8,128)(2,1)S(1)}, bf16[2048,2,128]{2,0,1:T(8,128)(2,1)}, u32[]{:S(2)}) copy-start(bf16[2048,2,128]{2,0,1:T(8,128)(2,1)} %get-tuple-element.362) | copy-start | bytes 3145732 | tf_op jit(solution)/shard_map/while
  305.5 3.2 copy-start.2
  313.8 9.4 %copy-start.10 = (bf16[2048,2,128]{2,0,1:T(8,128)(2,1)S(1)}, bf16[2048,2,128]{2,0,1:T(8,128)(2,1)}, u32[]{:S(2)}) copy-start(bf16[2048,2,128]{2,0,1:T(8,128)(2,1)} %get-tuple-element.362) | copy-start | bytes 3145732 | tf_op jit(solution)/shard_map/while
  337.1 3.2 copy-start.2
  345.4 9.4 %copy-start.10 = (bf16[2048,2,128]{2,0,1:T(8,128)(2,1)S(1)}, bf16[2048,2,128]{2,0,1:T(8,128)(2,1)}, u32[]{:S(2)}) copy-start(bf16[2048,2,128]{2,0,1:T(8,128)(2,1)} %get-tuple-element.362) | copy-start | bytes 3145732 | tf_op jit(solution)/shard_map/while
  376.5 78.7 %copy-start.7 = (bf16[256,2048]{1,0:T(8,128)(2,1)S(1)}, bf16[256,2048]{1,0:T(8,128)(2,1)}, u32[]{:S(2)}) copy-start(bf16[256,2048]{1,0:T(8,128)(2,1)} %param.20) | copy-start | bytes 3145732
  456.3 36.8 %copy-start.8 = (bf16[2048,256]{1,0:T(8,128)(2,1)S(1)}, bf16[2048,256]{1,0:T(8,128)(2,1)}, u32[]{:S(2)}) copy-start(bf16[2048,256]{1,0:T(8,128)(2,1)} %param.23) | copy-start | bytes 3145732
  456.3 16.1 %all-to-all-start.1 = ((bf16[8,128,256]{2,1,0:T(8,128)(2,1)}), bf16[8,128,256]{2,1,0:T(8,128)(2,1)S(1)}, u32[]{:S(2)}, u32[]{:S(2)}) async-start(bf16[8,128,256]{2,1,0:T(8,128)(2,1)} %bitcast.137), calls=%async_computation.2 | async-start | bytes 1048576 | tf_op jit(solution)/shard_map/all_to_all | solution.py:47
  463.1 30.4 %copy-start.9 = (bf16[2048,256]{1,0:T(8,128)(2,1)S(1)}, bf16[2048,256]{1,0:T(8,128)(2,1)}, u32[]{:S(2)}) copy-start(bf16[2048,256]{1,0:T(8,128)(2,1)} %param.22) | copy-start | bytes 3145732
  463.1 72.9 %all-gather.5.cloned.1.call-start = ((), (), s32[]{:S(2)}) async-start(), calls=%async_computation.8 | async-start | bytes 2228224 | tf_op jit(solution)/shard_map/all_gather | solution.py:69
  464.7 15.9 %copy-start.5 = (f32[2,128,256]{1,2,0:T(8,128)}, f32[2,128,256]{1,2,0:T(8,128)S(1)}, u32[]{:S(2)}) copy-start(f32[2,128,256]{1,2,0:T(8,128)S(1)} %fusion.35) | copy-start | bytes 786436
  539.1 2.0 copy-start.3
  549.7 20.2 %copy-start.11 = (bf16[2048,256]{0,1:T(8,128)(2,1)S(1)}, bf16[2048,256]{0,1:T(8,128)(2,1)}, u32[]{:S(2)}) copy-start(bf16[2048,256]{0,1:T(8,128)(2,1)} %get-tuple-element.247) | copy-start | bytes 3145732 | tf_op jit(solution)/shard_map/cond
  573.6 18.4 %copy-start.6 = (f32[2,128,256]{1,2,0:T(8,128)S(1)}, f32[2,128,256]{1,2,0:T(8,128)}, u32[]{:S(2)}) copy-start(f32[2,128,256]{1,2,0:T(8,128)} %copy-done.5) | copy-start | bytes 786436
  573.6 19.2 %copy-start.1 = (bf16[2048,256]{1,0:T(8,128)(2,1)S(1)}, bf16[2048,256]{1,0:T(8,128)(2,1)}, u32[]{:S(2)}) copy-start(bf16[2048,256]{1,0:T(8,128)(2,1)} %param.17) | copy-start | bytes 3145732
Sparse Core Ops, SparseCore 0:
  23.6 200.1 all-gather.2
  380.4 72.6 reduce-scatter.1
  494.7 41.2 all-gather.4
